TPU v7x, 32 devices: a whole 2x2x4 slice. The times are simulated.
32 devices in a mesh: depth: 8 (over z, x), rows: 4 (over y, core).
Axes of the slice: x: 2, y: 2, z: 4, core: 2. Of those that a mesh axis runs over, the one named last changes fastest.
Arguments:
- density: float32 [128, 64, 1024], P('depth', 'rows'), may hold values from 0 to 1
- bin_of_level: int32 [16], replicated, may hold values from 0 to 7
- absorb_bins: float32 [8], replicated, may hold values from 0.00234375 to 0.0625
- emit_bins: float32 [8], replicated, may hold values from 0.2 to 3
- occupancy: int32 [8, 4, 8], P('depth', 'rows'), may hold values 0 or 1
- col_offsets: int32 [1024], replicated, may hold values from 2 to 6
- row_offsets: int32 [64], P('rows'), may hold values from 2 to 6
Outputs:
- front_transmittance: float32 [8, 64, 1024], P('depth', 'rows')
- final_image: float32 [2, 64, 1024], P(None, 'rows')
All inputs are finite; a program needn't handle non-finite values. No bound on the sum of `occupancy` on one device may be relied on, other than what follows from the above.
Results may differ from a plain program's by a relative error of at most 0.0002.
Values sent between devices are 32-bit elements; how exact they have to be, the bound alone decides.
A program may use at most 64 MiB of HBM per device.

v0:
```python
import jax
import jax.numpy as jnp
from jax import lax
from jax.sharding import PartitionSpec as P


def from_behind(block, axis, distance):
    devices = range(lax.axis_size(axis))
    route = [(i - distance, i) for i in devices if i - distance in devices]
    return lax.ppermute(block, axis, route)


def resample_columns(mixed, col_offsets):
    fraction = col_offsets.astype(jnp.float32) / 8.0
    pad_shape = mixed.shape[:-1] + (1,)
    right_side = jnp.concatenate([mixed[..., 1:], jnp.zeros(pad_shape, jnp.float32)], -1)
    return (1.0 - fraction) * mixed + fraction * right_side


def tables(bin_of_level, absorb_bins, emit_bins):
    count_bins = absorb_bins.shape[0]
    onehot = (bin_of_level[:, None] == jnp.arange(count_bins, dtype=jnp.int32)[None, :]).astype(
        jnp.float32
    )
    return (jnp.sum(onehot * absorb_bins[None, :], 1), jnp.sum(onehot * emit_bins[None, :], 1))


def classify(sampled, absorb_level, emit_level):
    levels = absorb_level.shape[0]
    scaled = sampled * float(levels - 1)
    absorption = jnp.zeros(sampled.shape, jnp.float32)
    emission = jnp.zeros(sampled.shape, jnp.float32)
    for knot_index in range(levels):
        weight = jnp.maximum(0.0, 1.0 - jnp.abs(scaled - float(knot_index)))
        absorption = absorption + weight * absorb_level[knot_index]
        emission = emission + weight * emit_level[knot_index]
    return (absorption, emission)


def composite(absorption, emission):
    inclusive = jnp.cumsum(absorption, 0)
    exclusive = inclusive - absorption
    light = jnp.sum(jnp.exp(-exclusive) * (1.0 - jnp.exp(-absorption)) * emission, 0)
    return (light, inclusive[-1])


def on_device(density, bin_of_level, absorb_bins, emit_bins, occupancy, col_offsets, row_offsets):
    following = from_behind(density[:1], "depth", -1)
    extended = jnp.concatenate([density, following], 0)
    mid_depth = 0.5 * (extended[:-1] + extended[1:])
    row_below = from_behind(mid_depth[:, :1], "rows", -1)
    next_rows = jnp.concatenate([mid_depth[:, 1:], row_below], 1)
    frac_row = (row_offsets.astype(jnp.float32) / 8.0)[None, :, None]
    mixed = (1.0 - frac_row) * mid_depth + frac_row * next_rows
    sampled = resample_columns(mixed, col_offsets)
    absorb_level, emit_level = tables(bin_of_level, absorb_bins, emit_bins)
    occupied = occupancy[0, 0]
    absorption, emission = classify(sampled, absorb_level, emit_level)
    brick_mask = jnp.repeat(occupied.astype(jnp.float32), 128)
    absorption = absorption * brick_mask[None, None, :]
    light, depth_sum = composite(absorption, emission)
    position = lax.axis_index("depth")
    pieces = lax.all_gather(depth_sum[None], "depth", axis=0, tiled=True)
    shard_ids = jnp.arange(pieces.shape[0], dtype=jnp.int32)
    in_front = (shard_ids < position)[:, None, None]
    front_depth = jnp.sum(jnp.where(in_front, pieces, 0.0), 0)
    total_depth = jnp.sum(pieces, 0)
    front = jnp.exp(-front_depth)
    radiance = lax.psum(front * light, "depth")
    final_image = jnp.stack([radiance, jnp.exp(-total_depth)])
    return (front[None], final_image)


def solution(mesh):
    placed = (P("depth", "rows", None), P(), P(), P(), P("depth", "rows", None), P(), P("rows"))
    return jax.shard_map(
        on_device,
        mesh=mesh,
        in_specs=placed,
        out_specs=(P("depth", "rows", None), P(None, "rows", None)),
        check_vma=False,
    )
```

profile of v0, /device:TPU:0, one launch (start us, length us, event | category | flops | bytes accessed | tf_op | source)
XLA Modules:
  0.0 160.8 jit_solution(6802575559535258758)
XLA Ops:
  7.2 0.0 all-reduce.3.cloned.1.call-start
  7.2 0.8 slice.114
  8.1 0.0 copy-start.4
  8.1 1.4 collective-permute-start
  9.5 0.1 select_reduce_fusion.1
  9.6 0.0 copy-start.1
  9.6 0.7 fusion.59
  10.4 0.6 copy-done.6
  11.1 0.1 broadcast_bitcast_fusion
  11.1 0.7 fusion.58
  11.8 3.5 %collective-permute-done = f32[1,16,1024]{2,1,0:T(8,128)S(1)} collective-permute-done((f32[1,16,1024]{2,1,0:T(8,128)S(1)}, f32[1,16,1024]{2,1,0:T(8,128)S(1)}, u32[]{:S(2)}, u32[]{:S(2)}) %collective-permute-start) | collective-permute-done | bytes 65568 | tf_op jit(solution)/shard_map/ppermute | solution.py:10
  15.3 1.7 %fusion.3 = f32[16,16,1024]{2,1,0:T(8,128)S(1)} fusion(f32[16,16,1024]{2,1,0:T(8,128)} %param.7, f32[1,16,1024]{2,1,0:T(8,128)S(1)} %collective-permute-done), kind=kLoop, calls=%fused_computation.24 | loop fusion | flops 786432 | bytes 2162688 | tf_op jit(solution)/shard_map/mul | solution.py:50
  17.1 1.3 collective-permute-start.1
  18.4 0.1 slice.152
  18.6 1.7 %collective-permute-done.1 = f32[16,1,1024]{2,1,0:T(1,128)S(1)} collective-permute-done((f32[16,1,1024]{2,1,0:T(1,128)S(1)}, f32[16,1,1024]{2,1,0:T(1,128)S(1)}, u32[]{:S(2)}, u32[]{:S(2)}) %collective-permute-start.1) | collective-permute-done | bytes 65568 | tf_op jit(solution)/shard_map/ppermute | solution.py:10
  20.3 0.3 fusion.1
  20.6 0.3 slice.154
  21.0 28.9 %multiply_reduce_fusion = (f32[16,1024]{1,0:T(8,128)S(1)}, f32[16,16,1024]{2,1,0:T(8,128)S(1)}) fusion(f32[]{:T(128)} %bitcast.34, f32[]{:T(128)} %bitcast.33, f32[]{:T(128)} %bitcast.32, f32[]{:T(128)} %bitcast.31, f32[]{:T(128)} %bitcast.30, f32[]{:T(128)} %bitcast.29, f32[]{:T(128)} %bitcast.28, f32[]{:T(128)} %bitcast.27, f32[]{:T(128)} %bitcast.26, ...), kind=kOutput, calls=%fused_computation.4 | output fusion | flops 65781760 | bytes 3222656 | tf_op jit(solution)/shard_map/jit(cumsum)/reduce_window_sum | solution.py:41
  49.8 32.2 %all_gather.3 = f32[8,16,1024]{2,1,0:T(8,128)S(1)} all-gather(f32[1,16,1024]{2,1,0:T(8,128)S(1)} %slice.155), channel_id=1, replica_groups=mesh['depth'=8,'rows'=4] {'depth'}, dimensions={0}, use_global_device_ids=true | all-gather | bytes 589824 | tf_op jit(solution)/shard_map/all_gather | solution.py:63
  82.0 0.1 fusion.57
  82.1 0.7 multiply_bitcast_fusion
  82.8 0.0 all-reduce.3.cloned.1.call-update
  82.8 69.7 %all-reduce.3.cloned.1.call-done = f32[1,16,1024]{2,1,0:T(8,128)} async-done(((f32[1,16,1024]{2,1,0:T(8,128)}), f32[1,16,1024]{2,1,0:T(8,128)}) %all-reduce.3.cloned.1.call-update) | async-done | bytes 65552 | tf_op jit(solution)/shard_map/psum | solution.py:69
  152.5 1.5 pad_maximum_fusion.1
  (18 shorter events, 0.1 us)
Async XLA Ops:
  7.2 145.3 %all-reduce.3.cloned.1.call-start = ((), (), s32[]{:S(2)}) async-start(), calls=%async_computation | async-start | bytes 131072 | tf_op jit(solution)/shard_map/psum | solution.py:69
  8.1 1.5 copy-start.2
  8.1 1.5 copy-start.3
  8.1 1.5 copy-start.4
  8.1 7.2 %collective-permute-start = (f32[1,16,1024]{2,1,0:T(8,128)S(1)}, f32[1,16,1024]{2,1,0:T(8,128)S(1)}, u32[]{:S(2)}, u32[]{:S(2)}) collective-permute-start(f32[1,16,1024]{2,1,0:T(8,128)S(1)} %slice.114), channel_id=1, source_target_pairs={{4,0},{8,4},{12,8},{16,12},{20,16},{24,20},{28,24},{5,1},{9,5},{13... | collective-permute-start | bytes 196616 | tf_op jit(solution)/shard_map/ppermute | solution.py:10
  9.6 0.7 copy-start.5
  9.6 0.8 copy-start.1
  10.4 0.7 copy-start.6
  17.1 3.1 %collective-permute-start.1 = (f32[16,1,1024]{2,1,0:T(1,128)S(1)}, f32[16,1,1024]{2,1,0:T(1,128)S(1)}, u32[]{:S(2)}, u32[]{:S(2)}) collective-permute-start(f32[16,1,1024]{2,1,0:T(1,128)S(1)} %slice.153), channel_id=1, source_target_pairs={{1,0},{2,1},{3,2},{5,4},{6,5},{7,6},{9,8},{10,9},{11,10},{13,12},{... | collective-permute-start | bytes 196616 | tf_op jit(solution)/shard_map/ppermute | solution.py:10
  18.4 1.8 %copy-start = (f32[16,16,1024]{2,1,0:T(8,128)S(1)}, f32[16,16,1024]{2,1,0:T(8,128)}, u32[]{:S(2)}) copy-start(f32[16,16,1024]{2,1,0:T(8,128)} %param.7) | copy-start | bytes 3145732
Sparse Core Ops, SparseCore 0:
  82.9 69.5 all-reduce.2
where the time goes:
time: 161 us
  waiting for transfers between devices  74.8 us (46%)
  other arithmetic  33.3 us (21%)
  blocking collectives  32.2 us (20%)
  between operations  14.2 us (9%)
  local copies, waits for them, and re-layouts  3.52 us (2%)
  starting transfers between devices  2.75 us (2%)
    psum x1, waiting for transfers between devices, on_device(): radiance = lax.psum(front * light, 'depth')  69.7 us
    all_gather x1, blocking collectives, on_device(): pieces = lax.all_gather(depth_sum[None], 'depth', axis=0, tiled=True)  32.2 us
    another operation x1, other arithmetic, composite(): inclusive = jnp.cumsum(absorption, 0)  28.9 us
    ppermute x2, waiting for transfers between devices, from_behind(): return lax.ppermute(block, axis, route)  5.18 us
  transfers between devices with their start and end apart: 3, of which 3 were waited for; matrix products, arithmetic and copies ran while one was open for 1% of the time, Pallas kernels for 0%

commit v1 on v0

v1 whole, which is shorter than its diff:
```python
import functools
import math

import jax
import jax.numpy as jnp
from jax import lax
from jax.experimental import pallas as pl
from jax.experimental.pallas import tpu as pltpu
from jax.sharding import PartitionSpec as P

LANES = 128
SUB = 8
MESH = pl.DeviceIdType.MESH


def repeat(count, body):
    if count <= 16:
        for i in range(count):
            body(i)
    else:
        lax.fori_loop(0, count, lambda i, c: (body(i), c)[1], 0)


def kernel(
    n_depth,
    n_rows,
    dens_hbm,
    bins_ref,
    absorb_ref,
    emit_ref,
    occ_ref,
    col_ref,
    row_ref,
    front_ref,
    image_ref,
    dens,
    below,
    row_send,
    row_halo,
    corner_send,
    corner,
    parts,
    gathered,
    answers,
    results,
    load_sem,
    halo_send_sem,
    halo_recv_sem,
    part_send_sem,
    part_recv_sem,
    ans_send_sem,
    ans_recv_sem,
):
    slab, rows, cols = dens.shape
    owners = parts.shape[0]
    width = cols // owners
    tiles = cols // LANES
    row_tiles = rows // SUB
    levels = bins_ref.shape[0]
    d = lax.axis_index("depth")
    r = lax.axis_index("rows")

    def shifted(dd, dr):
        return (lax.rem(d + dd + n_depth, n_depth), lax.rem(r + dr + n_rows, n_rows))

    load = pltpu.make_async_copy(dens_hbm, dens, load_sem)
    load.start()

    barrier = pltpu.get_barrier_semaphore()
    for dd, dr in ((0, -1), (0, 1), (-1, -1), (1, 1)):
        pl.semaphore_signal(barrier, inc=1, device_id=shifted(dd, dr), device_id_type=MESH)

    def greet(i):
        pl.semaphore_signal(
            barrier, inc=1, device_id=(lax.rem(d + 1 + i, n_depth), r), device_id_type=MESH
        )

    repeat(n_depth - 1, greet)

    @pl.when(d == n_depth - 1)
    def _():
        below[...] = jnp.zeros_like(below)

    @pl.when(r == n_rows - 1)
    def _():
        row_halo[...] = jnp.zeros_like(row_halo)

    @pl.when(jnp.logical_or(d == n_depth - 1, r == n_rows - 1))
    def _():
        corner[...] = jnp.zeros_like(corner)

    lane = lax.broadcasted_iota(jnp.int32, (SUB, LANES), 1)
    sub = lax.broadcasted_iota(jnp.int32, (SUB, LANES), 0)
    to_log2 = -math.log2(math.e)
    absorb = [absorb_ref[bins_ref[k]] * to_log2 for k in range(levels)]
    emit = [emit_ref[bins_ref[k]] for k in range(levels)]

    def table(values):
        base = jnp.full((SUB, LANES), values[-1], jnp.float32)
        slope = jnp.zeros((SUB, LANES), jnp.float32)
        for k in range(levels - 1):
            step = values[k + 1] - values[k]
            base = jnp.where(lane == k, values[k] - step * float(k), base)
            slope = jnp.where(lane == k, step, slope)
        return base, slope

    a_base, a_slope = table(absorb)
    e_base, e_slope = table(emit)
    occ = [occ_ref[0, 0, (c * LANES) // (cols // occ_ref.shape[2])].astype(jnp.float32) for c in range(tiles)]

    def row_weights(t):
        frac = jnp.zeros((SUB, LANES), jnp.float32)
        for y in range(SUB):
            frac = jnp.where(sub == y, row_ref[t * SUB + y].astype(jnp.float32), frac)
        frac = frac / 8.0
        gain = 0.5 * float(levels - 1)
        return gain * (1.0 - frac), gain * frac

    def col_weights(c):
        frac = col_ref[0:1, c * LANES : (c + 1) * LANES].astype(jnp.float32) / 8.0
        frac = jnp.broadcast_to(frac, (SUB, LANES))
        keep = 1.0 - frac
        if c == tiles - 1:
            frac = jnp.where(lane == LANES - 1, 0.0, frac)
        return keep, frac

    def resampled(own, following, rw, cws):
        mixed = []
        for c in range(tiles):
            block = own(c)
            up = jnp.where(sub == SUB - 1, following(c), pltpu.roll(block, SUB - 1, 0))
            mixed.append(rw[0] * block + rw[1] * up)
        turned = [pltpu.roll(m, LANES - 1, 1) for m in mixed]
        out = []
        for c in range(tiles):
            right = jnp.where(lane == LANES - 1, turned[(c + 1) % tiles], turned[c])
            out.append(cws[c][0] * mixed[c] + cws[c][1] * right)
        return out

    def shade(prev, now, state):
        through, depth, light = state
        new_through, new_depth, new_light = [], [], []
        for c in range(tiles):
            scaled = prev[c] + now[c]
            level = scaled.astype(jnp.int32)
            pick = functools.partial(jnp.take_along_axis, indices=level, axis=1, mode="promise_in_bounds")
            absorbed = (pick(a_base) + pick(a_slope) * scaled) * occ[c]
            emitted = pick(e_base) + pick(e_slope) * scaled
            after = through[c] * jnp.exp2(absorbed)
            new_light.append(light[c] + (through[c] - after) * emitted)
            new_depth.append(depth[c] + absorbed)
            new_through.append(after)
        return new_through, new_depth, new_light

    cws = [col_weights(c) for c in range(tiles)]

    def tile_of(c):
        return slice(c * LANES, (c + 1) * LANES)

    def plane(z, t, rw):
        def own(c):
            return dens[z, t * SUB : (t + 1) * SUB, tile_of(c)]

        def following(c):
            if t + 1 < row_tiles:
                nxt = dens[z, (t + 1) * SUB : (t + 1) * SUB + 1, tile_of(c)]
            else:
                nxt = row_halo[z, 0:1, tile_of(c)]
            return jnp.broadcast_to(nxt, (SUB, LANES))

        return resampled(own, following, rw, cws)

    def last_plane(t, rw):
        def own(c):
            return below[t * SUB : (t + 1) * SUB, tile_of(c)]

        def following(c):
            if t + 1 < row_tiles:
                nxt = below[(t + 1) * SUB : (t + 1) * SUB + 1, tile_of(c)]
            else:
                nxt = corner[0:1, tile_of(c)]
            return jnp.broadcast_to(nxt, (SUB, LANES))

        return resampled(own, following, rw, cws)

    def march(t):
        rw = row_weights(t)
        ones = [jnp.ones((SUB, LANES), jnp.float32)] * tiles
        zeros = [jnp.zeros((SUB, LANES), jnp.float32)] * tiles

        def step(z, carry):
            prev, state = carry
            now = plane(z, t, rw)
            return now, shade(prev, now, state)

        return lax.fori_loop(1, slab, step, (plane(0, t, rw), (ones, zeros, zeros)))

    def finish(t, carry):
        prev, state = carry
        _, depth, light = shade(prev, last_plane(t, row_weights(t)), state)
        for c in range(tiles):
            j, at = (c * LANES) // width, (c * LANES) % width
            parts[j, 0, t * SUB : (t + 1) * SUB, at : at + LANES] = depth[c]
            parts[j, 1, t * SUB : (t + 1) * SUB, at : at + LANES] = light[c]

    load.wait()
    for z in range(slab):
        row_send[z] = dens[z, 0:1, :]
    corner_send[...] = dens[0, 0:1, :]

    pl.semaphore_wait(barrier, n_depth - 1 + 4)

    def halo(k, src, dst, dd, dr):
        return pltpu.make_async_remote_copy(
            src_ref=src,
            dst_ref=dst,
            send_sem=halo_send_sem.at[k],
            recv_sem=halo_recv_sem.at[k],
            device_id=shifted(dd, dr),
            device_id_type=MESH,
        )

    depth_copy = halo(0, dens.at[0], below, -1, 0)
    rows_copy = halo(1, row_send, row_halo, 0, -1)
    corner_copy = halo(2, corner_send, corner, -1, -1)
    sends = (
        (depth_copy, d > 0, d < n_depth - 1),
        (rows_copy, r > 0, r < n_rows - 1),
        (
            corner_copy,
            jnp.logical_and(d > 0, r > 0),
            jnp.logical_and(d < n_depth - 1, r < n_rows - 1),
        ),
    )
    for copy, sending, _ in sends:
        pl.when(sending)(copy.start)

    halves = [march(t) for t in range(row_tiles - 1)]
    pl.when(sends[1][2])(rows_copy.wait_recv)
    halves.append(march(row_tiles - 1))
    pl.when(sends[0][2])(depth_copy.wait_recv)
    pl.when(sends[2][2])(corner_copy.wait_recv)
    for t, carry in enumerate(halves):
        finish(t, carry)

    def part_copy(owner, source):
        return pltpu.make_async_remote_copy(
            src_ref=parts.at[owner],
            dst_ref=gathered.at[source],
            send_sem=part_send_sem.at[owner],
            recv_sem=part_recv_sem.at[source],
            device_id=(owner, r),
            device_id_type=MESH,
        )

    def other(i):
        return lax.rem(d + 1 + i, n_depth)

    def when_owner(index, body):
        if owners == n_depth:
            body()
        else:
            pl.when(index < owners)(body)

    def send_part(i):
        when_owner(other(i), lambda: part_copy(other(i), d).start())

    repeat(n_depth - 1, send_part)

    def answer_copy(target, owner):
        return pltpu.make_async_remote_copy(
            src_ref=answers.at[target],
            dst_ref=results.at[owner],
            send_sem=ans_send_sem.at[target],
            recv_sem=ans_recv_sem.at[owner],
            device_id=(target, r),
            device_id_type=MESH,
        )

    @functools.partial(when_owner, d)
    def _():
        gathered[pl.ds(d, 1)] = parts[pl.ds(d, 1)]

        def arrived(i):
            part_copy(d, other(i)).wait_recv()

        repeat(n_depth - 1, arrived)

        def compose(i, carry):
            total, radiance = carry
            front = jnp.exp2(total)
            answers[i, 0] = front
            return total + gathered[i, 0], radiance + front * gathered[i, 1]

        zero = jnp.zeros((rows, width), jnp.float32)
        carry = (zero, zero)
        if n_depth <= 16:
            for i in range(n_depth):
                carry = compose(i, carry)
        else:
            carry = lax.fori_loop(0, n_depth, compose, carry)
        total, radiance = carry
        remaining = jnp.exp2(total)

        def fill(i):
            answers[i, 1] = radiance
            answers[i, 2] = remaining

        repeat(n_depth, fill)

        def reply(i):
            answer_copy(other(i), d).start()

        repeat(n_depth - 1, reply)
        results[pl.ds(d, 1)] = answers[pl.ds(d, 1)]

    def collect(i):
        when_owner(other(i), lambda: answer_copy(d, other(i)).wait_recv())

    repeat(n_depth - 1, collect)
    for j in range(owners):
        where = slice(j * width, (j + 1) * width)
        front_ref[0, :, where] = results[j, 0]
        image_ref[0, :, where] = results[j, 1]
        image_ref[1, :, where] = results[j, 2]

    for copy, sending, _ in sends:
        pl.when(sending)(copy.wait_send)

    def sent(i):
        when_owner(other(i), lambda: part_copy(other(i), d).wait_send())
        when_owner(d, lambda: answer_copy(other(i), d).wait_send())

    repeat(n_depth - 1, sent)


def on_device(n_depth, n_rows, density, bin_of_level, absorb_bins, emit_bins, occupancy, col_offsets, row_offsets):
    slab, rows, cols = density.shape
    owners = 1
    while owners * 2 <= n_depth and cols % (owners * 2 * LANES) == 0:
        owners *= 2
    width = cols // owners
    smem = pl.BlockSpec(memory_space=pltpu.SMEM)
    vmem = pl.BlockSpec(memory_space=pltpu.VMEM)
    f32 = jnp.float32
    return pl.pallas_call(
        functools.partial(kernel, n_depth, n_rows),
        out_shape=(
            jax.ShapeDtypeStruct((1, rows, cols), f32),
            jax.ShapeDtypeStruct((2, rows, cols), f32),
        ),
        in_specs=[pl.BlockSpec(memory_space=pl.ANY), smem, smem, smem, smem, vmem, smem],
        out_specs=(vmem, vmem),
        scratch_shapes=[
            pltpu.VMEM((slab, rows, cols), f32),
            pltpu.VMEM((rows, cols), f32),
            pltpu.VMEM((slab, 1, cols), f32),
            pltpu.VMEM((slab, 1, cols), f32),
            pltpu.VMEM((1, cols), f32),
            pltpu.VMEM((1, cols), f32),
            pltpu.VMEM((owners, 2, rows, width), f32),
            pltpu.VMEM((n_depth, 2, rows, width), f32),
            pltpu.VMEM((n_depth, 3, rows, width), f32),
            pltpu.VMEM((owners, 3, rows, width), f32),
            pltpu.SemaphoreType.DMA,
            pltpu.SemaphoreType.DMA((3,)),
            pltpu.SemaphoreType.DMA((3,)),
            pltpu.SemaphoreType.DMA((owners,)),
            pltpu.SemaphoreType.DMA((n_depth,)),
            pltpu.SemaphoreType.DMA((n_depth,)),
            pltpu.SemaphoreType.DMA((owners,)),
        ],
        compiler_params=pltpu.CompilerParams(collective_id=0, has_side_effects=True),
    )(
        density,
        bin_of_level,
        absorb_bins,
        emit_bins,
        occupancy,
        col_offsets.reshape(1, cols),
        row_offsets,
    )


def solution(mesh):
    placed = (P("depth", "rows", None), P(), P(), P(), P("depth", "rows", None), P(), P("rows"))
    return jax.shard_map(
        functools.partial(on_device, mesh.shape["depth"], mesh.shape["rows"]),
        mesh=mesh,
        in_specs=placed,
        out_specs=(P("depth", "rows", None), P(None, "rows", None)),
        check_vma=False,
    )
```

time: 161 us -> 28.2 us (0.18)
  waiting for transfers between devices: 74.8 us -> 0 us
  other arithmetic: 33.3 us -> 0 us
  blocking collectives: 32.2 us -> 0 us
  Pallas kernels: 0 us -> 25.2 us
  between operations: 14.2 us -> 0.65 us
  starting transfers between devices: 2.75 us -> 0 us
    psum x1 -> x0, waiting for transfers between devices: 69.7 us -> none  [on_device(): radiance = lax.psum(front * light, 'depth')]
    all_gather x1 -> x0, blocking collectives: 32.2 us -> none  [on_device(): pieces = lax.all_gather(depth_sum[None], 'depth', axis=0, tiled=True)]
    another operation x3 -> x0, other arithmetic: 31 us -> none  [the longest x1 28.9 us: composite(): inclusive = jnp.cumsum(absorption, 0)]
    pallas_call x0 -> x1, Pallas kernels: none -> 25.2 us  [on_device(): pl.pallas_call(functools.partial(kernel, n_depth, n_rows), out_shape=(jax...]
    ppermute x2 -> x0, waiting for transfers between devices: 5.18 us -> none  [from_behind(): return lax.ppermute(block, axis, route)]
    slice x7 -> x0, local copies, waits for them, and re-layouts: 2.78 us -> none  [the longest x1 0.85 us: on_device(): following = from_behind(density[:1], 'depth', -1)]
    ppermute x2 -> x0, starting transfers between devices: 2.72 us -> none  [from_behind(): return lax.ppermute(block, axis, route)]
    mul x2 -> x0, other arithmetic: 1.75 us -> none  [the longest x1 1.74 us: on_device(): mid_depth = 0.5 * (extended[:-1] + extended[1:])]
  transfers between devices with their start and end apart: 3 -> 0, of which waited for: 3 -> 0; matrix products, arithmetic and copies ran while one was open for 1% -> 0% of each run, Pallas kernels for 0% -> 0%
where the time goes in v1:
time: 28.2 us; the launch traced here: 28 us
  Pallas kernels  25.2 us (89%)
  local copies, waits for them, and re-layouts  2.17 us (8%)
  between operations  0.65 us (2%)
    pallas_call x1, Pallas kernels, on_device(): pl.pallas_call(functools.partial(kernel, n_depth, n_rows), out_shape=(jax...  25.2 us
    unnamed x4, local copies, waits for them, and re-layouts  2.17 us

profile of v1, /device:TPU:0, one launch (start us, length us, event | category | flops | bytes accessed | tf_op | source)
XLA Modules:
  0.0 28.0 jit_solution(1962580558011657872)
XLA Ops:
  0.6 25.2 %shard_map.86 = (f32[1,16,1024]{2,1,0:T(8,128)}, f32[2,16,1024]{2,1,0:T(8,128)}) custom-call(f32[16,16,1024]{2,1,0:T(8,128)} %dens_hbm.1, s32[16]{0:T(128)} %bins_ref.1, f32[8]{0:T(128)} %absorb_ref.1, f32[8]{0:T(128)} %emit_ref.1, s32[1,1,8]{2,1,0:T(1,128)} %occ_ref.1, s32[1,1024]{1,0:T(1,128)} %bitcast.1, s32[16]{0:T(128)} %row_ref.1), custom_call_target="tpu_custom_call" | custom-call | tf_op jit(solution)/shard_map/pallas_call | solution.py:346
  25.9 0.0 copy-start
  25.9 1.5 %copy.11 = f32[1,16,1024]{2,1,0:T(8,128)} copy(f32[1,16,1024]{2,1,0:T(8,128)} %get-tuple-element.4) | data formatting | bytes 131072
  27.4 0.0 copy-done
  27.4 0.7 %copy.12 = f32[2,16,1024]{2,1,0:T(8,128)} copy(f32[2,16,1024]{2,1,0:T(8,128)S(1)} %copy-done) | data formatting | bytes 262144
Async XLA Ops:
  25.9 1.5 %copy-start = (f32[2,16,1024]{2,1,0:T(8,128)S(1)}, f32[2,16,1024]{2,1,0:T(8,128)}, u32[]{:S(2)}) copy-start(f32[2,16,1024]{2,1,0:T(8,128)} %get-tuple-element.5) | copy-start | bytes 393220

commit v2 on v1

--- a/solution.py
+++ b/solution.py
@@ -31,8 +31,7 @@
     occ_ref,
     col_ref,
     row_ref,
-    front_ref,
-    image_ref,
+    results,
     dens,
     below,
     row_send,
@@ -42,7 +41,6 @@
     parts,
     gathered,
     answers,
-    results,
     load_sem,
     halo_send_sem,
     halo_recv_sem,
@@ -52,7 +50,7 @@
     ans_recv_sem,
 ):
     slab, rows, cols = dens.shape
-    owners = parts.shape[0]
+    owners = parts.shape[1]
     width = cols // owners
     tiles = cols // LANES
     row_tiles = rows // SUB
@@ -95,17 +93,16 @@
     absorb = [absorb_ref[bins_ref[k]] * to_log2 for k in range(levels)]
     emit = [emit_ref[bins_ref[k]] for k in range(levels)]
 
-    def table(values):
-        base = jnp.full((SUB, LANES), values[-1], jnp.float32)
-        slope = jnp.zeros((SUB, LANES), jnp.float32)
-        for k in range(levels - 1):
-            step = values[k + 1] - values[k]
-            base = jnp.where(lane == k, values[k] - step * float(k), base)
-            slope = jnp.where(lane == k, step, slope)
-        return base, slope
-
-    a_base, a_slope = table(absorb)
-    e_base, e_slope = table(emit)
+    def hinges(values):
+        steps = [values[k + 1] - values[k] for k in range(levels - 1)]
+        bend = steps[:1] + [steps[k] - steps[k - 1] for k in range(1, levels - 1)]
+        shift = values[0]
+        for k in range(1, levels - 1):
+            shift = shift - bend[k] * float(k)
+        return shift, bend
+
+    a_shift, a_bend = hinges(absorb)
+    e_shift, e_bend = hinges(emit)
     occ = [occ_ref[0, 0, (c * LANES) // (cols // occ_ref.shape[2])].astype(jnp.float32) for c in range(tiles)]
 
     def row_weights(t):
@@ -142,10 +139,13 @@
         new_through, new_depth, new_light = [], [], []
         for c in range(tiles):
             scaled = prev[c] + now[c]
-            level = scaled.astype(jnp.int32)
-            pick = functools.partial(jnp.take_along_axis, indices=level, axis=1, mode="promise_in_bounds")
-            absorbed = (pick(a_base) + pick(a_slope) * scaled) * occ[c]
-            emitted = pick(e_base) + pick(e_slope) * scaled
+            absorbed = a_shift + a_bend[0] * scaled
+            emitted = e_shift + e_bend[0] * scaled
+            for k in range(1, levels - 1):
+                hinge = jnp.maximum(scaled, float(k))
+                absorbed = absorbed + a_bend[k] * hinge
+                emitted = emitted + e_bend[k] * hinge
+            absorbed = absorbed * occ[c]
             after = through[c] * jnp.exp2(absorbed)
             new_light.append(light[c] + (through[c] - after) * emitted)
             new_depth.append(depth[c] + absorbed)
@@ -183,30 +183,35 @@
 
         return resampled(own, following, rw, cws)
 
-    def march(t):
+    def march(t, first, last, carry):
         rw = row_weights(t)
-        ones = [jnp.ones((SUB, LANES), jnp.float32)] * tiles
-        zeros = [jnp.zeros((SUB, LANES), jnp.float32)] * tiles
+        if carry is None:
+            ones = [jnp.ones((SUB, LANES), jnp.float32)] * tiles
+            zeros = [jnp.zeros((SUB, LANES), jnp.float32)] * tiles
+            carry = (plane(0, t, rw), (ones, zeros, zeros))
 
         def step(z, carry):
             prev, state = carry
             now = plane(z, t, rw)
             return now, shade(prev, now, state)
 
-        return lax.fori_loop(1, slab, step, (plane(0, t, rw), (ones, zeros, zeros)))
+        return lax.fori_loop(first, last, step, carry)
 
     def finish(t, carry):
         prev, state = carry
         _, depth, light = shade(prev, last_plane(t, row_weights(t)), state)
         for c in range(tiles):
             j, at = (c * LANES) // width, (c * LANES) % width
-            parts[j, 0, t * SUB : (t + 1) * SUB, at : at + LANES] = depth[c]
-            parts[j, 1, t * SUB : (t + 1) * SUB, at : at + LANES] = light[c]
+            parts[t, j, 0, :, at : at + LANES] = depth[c]
+            parts[t, j, 1, :, at : at + LANES] = light[c]
 
     load.wait()
     for z in range(slab):
         row_send[z] = dens[z, 0:1, :]
     corner_send[...] = dens[0, 0:1, :]
+    half = slab // 2
+    states = [None] * row_tiles
+    states[0] = march(0, 1, half, None)
 
     pl.semaphore_wait(barrier, n_depth - 1 + 4)
 
@@ -235,24 +240,6 @@
     for copy, sending, _ in sends:
         pl.when(sending)(copy.start)
 
-    halves = [march(t) for t in range(row_tiles - 1)]
-    pl.when(sends[1][2])(rows_copy.wait_recv)
-    halves.append(march(row_tiles - 1))
-    pl.when(sends[0][2])(depth_copy.wait_recv)
-    pl.when(sends[2][2])(corner_copy.wait_recv)
-    for t, carry in enumerate(halves):
-        finish(t, carry)
-
-    def part_copy(owner, source):
-        return pltpu.make_async_remote_copy(
-            src_ref=parts.at[owner],
-            dst_ref=gathered.at[source],
-            send_sem=part_send_sem.at[owner],
-            recv_sem=part_recv_sem.at[source],
-            device_id=(owner, r),
-            device_id_type=MESH,
-        )
-
     def other(i):
         return lax.rem(d + 1 + i, n_depth)
 
@@ -262,76 +249,112 @@
         else:
             pl.when(index < owners)(body)
 
-    def send_part(i):
-        when_owner(other(i), lambda: part_copy(other(i), d).start())
-
-    repeat(n_depth - 1, send_part)
-
-    def answer_copy(target, owner):
+    def part_copy(t, owner, source):
         return pltpu.make_async_remote_copy(
-            src_ref=answers.at[target],
-            dst_ref=results.at[owner],
-            send_sem=ans_send_sem.at[target],
-            recv_sem=ans_recv_sem.at[owner],
+            src_ref=parts.at[t, owner],
+            dst_ref=gathered.at[t, source],
+            send_sem=part_send_sem.at[t, owner],
+            recv_sem=part_recv_sem.at[t, source],
+            device_id=(owner, r),
+            device_id_type=MESH,
+        )
+
+    def answer_copy(t, target, owner):
+        return pltpu.make_async_remote_copy(
+            src_ref=answers.at[t, target],
+            dst_ref=results.at[t, owner],
+            send_sem=ans_send_sem.at[t, target],
+            recv_sem=ans_recv_sem.at[t, owner],
             device_id=(target, r),
             device_id_type=MESH,
         )
 
-    @functools.partial(when_owner, d)
-    def _():
-        gathered[pl.ds(d, 1)] = parts[pl.ds(d, 1)]
+    def send_parts(t):
+        def send(i):
+            when_owner(other(i), lambda: part_copy(t, other(i), d).start())
+
+        repeat(n_depth - 1, send)
+
+    def compose(t):
+        gathered[t, pl.ds(d, 1)] = parts[t, pl.ds(d, 1)]
 
         def arrived(i):
-            part_copy(d, other(i)).wait_recv()
+            part_copy(t, d, other(i)).wait_recv()
 
         repeat(n_depth - 1, arrived)
 
-        def compose(i, carry):
+        def add(i, carry):
             total, radiance = carry
             front = jnp.exp2(total)
-            answers[i, 0] = front
-            return total + gathered[i, 0], radiance + front * gathered[i, 1]
-
-        zero = jnp.zeros((rows, width), jnp.float32)
+            answers[t, i, 0] = front
+            return total + gathered[t, i, 0], radiance + front * gathered[t, i, 1]
+
+        zero = jnp.zeros((SUB, width), jnp.float32)
         carry = (zero, zero)
         if n_depth <= 16:
             for i in range(n_depth):
-                carry = compose(i, carry)
+                carry = add(i, carry)
         else:
-            carry = lax.fori_loop(0, n_depth, compose, carry)
+            carry = lax.fori_loop(0, n_depth, add, carry)
         total, radiance = carry
         remaining = jnp.exp2(total)
 
         def fill(i):
-            answers[i, 1] = radiance
-            answers[i, 2] = remaining
+            answers[t, i, 1] = radiance
+            answers[t, i, 2] = remaining
 
         repeat(n_depth, fill)
 
         def reply(i):
-            answer_copy(other(i), d).start()
+            answer_copy(t, other(i), d).start()
 
         repeat(n_depth - 1, reply)
-        results[pl.ds(d, 1)] = answers[pl.ds(d, 1)]
-
-    def collect(i):
-        when_owner(other(i), lambda: answer_copy(d, other(i)).wait_recv())
-
-    repeat(n_depth - 1, collect)
-    for j in range(owners):
-        where = slice(j * width, (j + 1) * width)
-        front_ref[0, :, where] = results[j, 0]
-        image_ref[0, :, where] = results[j, 1]
-        image_ref[1, :, where] = results[j, 2]
+        results[t, pl.ds(d, 1)] = answers[t, pl.ds(d, 1)]
+
+    states[0] = march(0, half, slab, states[0])
+    pl.when(sends[1][2])(rows_copy.wait_recv)
+    for t in range(row_tiles):
+        last = t == row_tiles - 1
+        if not last:
+            states[t + 1] = march(t + 1, 1, half, None)
+        if t == 0:
+            pl.when(sends[0][2])(depth_copy.wait_recv)
+            pl.when(sends[2][2])(corner_copy.wait_recv)
+        finish(t, states[t])
+        send_parts(t)
+        if not last:
+            states[t + 1] = march(t + 1, half, slab, states[t + 1])
+
+    for t in range(row_tiles):
+        when_owner(d, functools.partial(compose, t))
+
+    for t in range(row_tiles):
+
+        def collect(i):
+            when_owner(other(i), lambda: answer_copy(t, d, other(i)).wait_recv())
+
+        repeat(n_depth - 1, collect)
 
     for copy, sending, _ in sends:
         pl.when(sending)(copy.wait_send)
 
-    def sent(i):
-        when_owner(other(i), lambda: part_copy(other(i), d).wait_send())
-        when_owner(d, lambda: answer_copy(other(i), d).wait_send())
-
-    repeat(n_depth - 1, sent)
+    for t in range(row_tiles):
+
+        def sent(i):
+            when_owner(other(i), lambda: part_copy(t, other(i), d).wait_send())
+            when_owner(d, lambda: answer_copy(t, other(i), d).wait_send())
+
+        repeat(n_depth - 1, sent)
+
+
+def lay_out(results, front_ref, image_ref):
+    row_tiles, owners, _, _, width = results.shape
+    for t in range(row_tiles):
+        for j in range(owners):
+            tall, where = slice(t * SUB, (t + 1) * SUB), slice(j * width, (j + 1) * width)
+            front_ref[0, tall, where] = results[t, j, 0]
+            image_ref[0, tall, where] = results[t, j, 1]
+            image_ref[1, tall, where] = results[t, j, 2]
 
 
 def on_device(n_depth, n_rows, density, bin_of_level, absorb_bins, emit_bins, occupancy, col_offsets, row_offsets):
@@ -340,17 +363,15 @@
     while owners * 2 <= n_depth and cols % (owners * 2 * LANES) == 0:
         owners *= 2
     width = cols // owners
+    row_tiles = rows // SUB
     smem = pl.BlockSpec(memory_space=pltpu.SMEM)
     vmem = pl.BlockSpec(memory_space=pltpu.VMEM)
     f32 = jnp.float32
-    return pl.pallas_call(
+    results = pl.pallas_call(
         functools.partial(kernel, n_depth, n_rows),
-        out_shape=(
-            jax.ShapeDtypeStruct((1, rows, cols), f32),
-            jax.ShapeDtypeStruct((2, rows, cols), f32),
-        ),
+        out_shape=pltpu.VMEM((row_tiles, owners, 3, SUB, width), f32),
         in_specs=[pl.BlockSpec(memory_space=pl.ANY), smem, smem, smem, smem, vmem, smem],
-        out_specs=(vmem, vmem),
+        out_specs=vmem,
         scratch_shapes=[
             pltpu.VMEM((slab, rows, cols), f32),
             pltpu.VMEM((rows, cols), f32),
@@ -358,17 +379,16 @@
             pltpu.VMEM((slab, 1, cols), f32),
             pltpu.VMEM((1, cols), f32),
             pltpu.VMEM((1, cols), f32),
-            pltpu.VMEM((owners, 2, rows, width), f32),
-            pltpu.VMEM((n_depth, 2, rows, width), f32),
-            pltpu.VMEM((n_depth, 3, rows, width), f32),
-            pltpu.VMEM((owners, 3, rows, width), f32),
+            pltpu.VMEM((row_tiles, owners, 2, SUB, width), f32),
+            pltpu.VMEM((row_tiles, n_depth, 2, SUB, width), f32),
+            pltpu.VMEM((row_tiles, n_depth, 3, SUB, width), f32),
             pltpu.SemaphoreType.DMA,
             pltpu.SemaphoreType.DMA((3,)),
             pltpu.SemaphoreType.DMA((3,)),
-            pltpu.SemaphoreType.DMA((owners,)),
-            pltpu.SemaphoreType.DMA((n_depth,)),
-            pltpu.SemaphoreType.DMA((n_depth,)),
-            pltpu.SemaphoreType.DMA((owners,)),
+            pltpu.SemaphoreType.DMA((row_tiles, owners)),
+            pltpu.SemaphoreType.DMA((row_tiles, n_depth)),
+            pltpu.SemaphoreType.DMA((row_tiles, n_depth)),
+            pltpu.SemaphoreType.DMA((row_tiles, owners)),
         ],
         compiler_params=pltpu.CompilerParams(collective_id=0, has_side_effects=True),
     )(
@@ -380,6 +400,8 @@
         col_offsets.reshape(1, cols),
         row_offsets,
     )
+    laid = results.transpose(2, 0, 3, 1, 4).reshape(3, rows, cols)
+    return laid[:1], laid[1:]
 
 
 def solution(mesh):

time: 28.2 us -> 23.7 us (0.84)
  Pallas kernels: 25.2 us -> 21.5 us
  local copies, waits for them, and re-layouts: 2.17 us -> 1.37 us
    pallas_call x1, Pallas kernels: 25.2 us -> 21.5 us  [on_device(): pl.pallas_call(functools.partial(kernel, n_depth, n_rows), out_shape=pltp...]
    unnamed x4 -> x0, local copies, waits for them, and re-layouts: 2.17 us -> none
    slice x0 -> x4, local copies, waits for them, and re-layouts: none -> 1.37 us  [on_device(): return (laid[:1], laid[1:])]
where the time goes in v2:
time: 23.7 us; the launch traced here: 23.5 us
  Pallas kernels  21.5 us (91%)
  local copies, waits for them, and re-layouts  1.37 us (6%)
  between operations  0.65 us (3%)
    pallas_call x1, Pallas kernels, on_device(): pl.pallas_call(functools.partial(kernel, n_depth, n_rows), out_shape=pltp...  21.5 us
    slice x4, local copies, waits for them, and re-layouts, on_device(): return (laid[:1], laid[1:])  1.37 us

profile of v2, /device:TPU:0, one launch (start us, length us, event | category | flops | bytes accessed | tf_op | source)
XLA Modules:
  0.0 23.5 jit_solution(11414684008539108653)
XLA Ops:
  0.6 21.5 %shard_map.86 = f32[2,8,3,8,128]{4,3,2,1,0:T(8,128)S(1)} custom-call(f32[16,16,1024]{2,1,0:T(8,128)} %dens_hbm.1, s32[16]{0:T(128)} %bins_ref.1, f32[8]{0:T(128)} %absorb_ref.1, f32[8]{0:T(128)} %emit_ref.1, s32[1,1,8]{2,1,0:T(1,128)} %occ_ref.1, s32[1,1024]{1,0:T(1,128)} %bitcast.8, s32[16]{0:T(128)} %row_ref.1), custom_call_target="tpu_custom_call" | custom-call | tf_op jit(solution)/shard_map/pallas_call | solution.py:370
  22.1 0.6 %slice_bitcast_fusion = f32[1,16,1024]{2,1,0:T(8,128)} fusion(f32[3,2,8,8,128]{4,2,0,3,1:T(8,128)S(1)} %bitcast.6), kind=kLoop, calls=%fused_computation | loop fusion | bytes 131072 | tf_op jit(solution)/shard_map/slice | solution.py:404
  22.8 0.7 %slice.15 = f32[2,16,1024]{2,1,0:T(8,128)} reshape(f32[2,2,8,8,128]{4,3,2,1,0:T(8,128)S(1)} %copy.9) | data formatting | bytes 262144 | tf_op jit(solution)/shard_map/slice | solution.py:404
  (2 shorter events, 0.1 us)

commit v3 on v2

--- a/solution.py
+++ b/solution.py
@@ -316,14 +316,14 @@
     for t in range(row_tiles):
         last = t == row_tiles - 1
         if not last:
-            states[t + 1] = march(t + 1, 1, half, None)
+            states[t + 1] = march(t + 1, 1, slab // 4, None)
         if t == 0:
             pl.when(sends[0][2])(depth_copy.wait_recv)
             pl.when(sends[2][2])(corner_copy.wait_recv)
         finish(t, states[t])
         send_parts(t)
         if not last:
-            states[t + 1] = march(t + 1, half, slab, states[t + 1])
+            states[t + 1] = march(t + 1, slab // 4, slab, states[t + 1])
 
     for t in range(row_tiles):
         when_owner(d, functools.partial(compose, t))

time: 23.7 us -> 24.4 us (1.030)
  Pallas kernels: 21.5 us -> 22.2 us
    pallas_call x1, Pallas kernels: 21.5 us -> 22.2 us  [on_device(): pl.pallas_call(functools.partial(kernel, n_depth, n_rows), out_shape=pltp...]
where the time goes in v3:
time: 24.4 us; the launch traced here: 24.2 us
  Pallas kernels  22.2 us (91%)
  local copies, waits for them, and re-layouts  1.37 us (6%)
  between operations  0.65 us (3%)
    pallas_call x1, Pallas kernels, on_device(): pl.pallas_call(functools.partial(kernel, n_depth, n_rows), out_shape=pltp...  22.2 us
    slice x4, local copies, waits for them, and re-layouts, on_device(): return (laid[:1], laid[1:])  1.37 us

profile of v3, /device:TPU:0, one launch (start us, length us, event | category | flops | bytes accessed | tf_op | source)
XLA Modules:
  0.0 24.2 jit_solution(2555896305172246850)
XLA Ops:
  0.6 22.2 %shard_map.86 = f32[2,8,3,8,128]{4,3,2,1,0:T(8,128)S(1)} custom-call(f32[16,16,1024]{2,1,0:T(8,128)} %dens_hbm.1, s32[16]{0:T(128)} %bins_ref.1, f32[8]{0:T(128)} %absorb_ref.1, f32[8]{0:T(128)} %emit_ref.1, s32[1,1,8]{2,1,0:T(1,128)} %occ_ref.1, s32[1,1024]{1,0:T(1,128)} %bitcast.8, s32[16]{0:T(128)} %row_ref.1), custom_call_target="tpu_custom_call" | custom-call | tf_op jit(solution)/shard_map/pallas_call | solution.py:370
  22.8 0.6 %slice_bitcast_fusion = f32[1,16,1024]{2,1,0:T(8,128)} fusion(f32[3,2,8,8,128]{4,2,0,3,1:T(8,128)S(1)} %bitcast.6), kind=kLoop, calls=%fused_computation | loop fusion | bytes 131072 | tf_op jit(solution)/shard_map/slice | solution.py:404
  23.5 0.7 %slice.15 = f32[2,16,1024]{2,1,0:T(8,128)} reshape(f32[2,2,8,8,128]{4,3,2,1,0:T(8,128)S(1)} %copy.9) | data formatting | bytes 262144 | tf_op jit(solution)/shard_map/slice | solution.py:404
  (2 shorter events, 0.1 us)
